TPU v7x, 32 devices: a whole 2x2x4 slice. The times are simulated.
32 devices in a mesh: seq: 8 (over z, x), head: 4 (over y, core).
Axes of the slice: x: 2, y: 2, z: 4, core: 2. Of those that a mesh axis runs over, the one named last changes fastest.
Arguments:
- prompt_queries: bfloat16 [1536, 4096], P('seq', 'head'), may hold values from -16 to 16
- prompt_keys: bfloat16 [1536, 1024], P('seq', 'head'), may hold values from -16 to 16
- prompt_values: bfloat16 [1536, 1024], P('seq', 'head'), may hold values from -6 to 6
- span_offset: int32 [8], P('seq'), may hold values from 0 to 7, each once
- appended_queries: bfloat16 [8, 4096], P(None, 'head'), may hold values from -16 to 16
- appended_keys: bfloat16 [8, 1024], P(None, 'head'), may hold values from -6 to 6
- appended_values: bfloat16 [8, 1024], P(None, 'head'), may hold values from -6 to 6
- dec_pos: int32 [8], replicated, may hold values from 2 to 1536, as said below
- out_weight: bfloat16 [4096, 4096], P('head'), may hold values from -0.09375 to 0.09375
Outputs:
- layer_out: bfloat16 [1536, 4096], P(('seq', 'head'))
- dec_out: bfloat16 [8, 4096], P('seq', 'head')
Inputs may be any that keep to these rules, and one draw needn't show every extreme that they name: span_offset is a permutation of 0 to 7. `dec_pos`: some appended token stands at 1536 in every draw.
All inputs are finite; a program needn't handle non-finite values.
Results may differ from a plain program's by a relative error of at most 0.015.
Values may be sent and summed in bfloat16 or wider, within the bound.
A program may use at most 256 MiB of HBM per device.

v0:
```python
from functools import partial

import jax
import jax.numpy as jnp
from jax import lax
from jax.sharding import PartitionSpec as P

QUERY_HEADS = 32
KEY_VALUE_HEADS = 8
HEAD_SIZE = 128


masked_score = -1e30


def lookup(lookup_table, index):
    slots = jnp.arange(lookup_table.shape[0], dtype=jnp.int32)
    return jnp.sum(
        lookup_table[None, :] * (index[:, None] == slots[None, :]).astype(jnp.int32), axis=1
    )


def piece_update(state, query_rows, query_pos, key_rows, value_rows, key_pos, score_scale):
    run_max, run_sum, run_acc = state
    scores = (
        jnp.einsum("rkgd,skd->rkgs", query_rows, key_rows, preferred_element_type=jnp.float32)
        * score_scale
    )
    allowed = (key_pos[None, :] <= query_pos[:, None])[:, None, None, :]
    piece_max = jnp.max(jnp.where(allowed, scores, masked_score), axis=-1)
    new_max = jnp.maximum(run_max, piece_max)
    weights = jnp.where(allowed, jnp.exp(scores - new_max[..., None]), 0.0)
    run_sum = jnp.sum(weights, axis=-1)
    added = jnp.einsum(
        "rkgs,skd->rkgd",
        weights.astype(jnp.bfloat16),
        value_rows,
        preferred_element_type=jnp.float32,
    )
    run_acc = added
    return (new_max, run_sum, run_acc)


def unchanged(state):
    return state


def finish(state):
    return state[2] / state[1][..., None]


def on_device(
    prompt_queries,
    prompt_keys,
    prompt_values,
    span_offset,
    appended_queries,
    appended_keys,
    appended_values,
    dec_pos,
    out_weight,
):
    tok_rows = prompt_queries.shape[0]
    kv_heads = prompt_keys.shape[1] // HEAD_SIZE
    group_width = QUERY_HEADS // KEY_VALUE_HEADS
    row_width = prompt_queries.shape[1]
    score_scale = HEAD_SIZE ** (-0.5)
    seq_count = lax.axis_size("seq")
    seq_index = lax.axis_index("seq")
    offs_all = lax.all_gather(span_offset, "seq", axis=0, tiled=True)
    own_offset = span_offset[0]
    row_ids = jnp.arange(tok_rows, dtype=jnp.int32)
    query_pos = own_offset * tok_rows + row_ids
    block_count = 1
    block_rows = tok_rows // block_count
    queries = prompt_queries.reshape(tok_rows, kv_heads, group_width, HEAD_SIZE)
    block_q = [queries]
    block_pos = [query_pos]
    block_top = [jnp.max(positions) for positions in block_pos]
    start_state = tuple(
        (
            (
                jnp.full((block_rows, kv_heads, group_width), masked_score, jnp.float32),
                jnp.zeros((block_rows, kv_heads, group_width), jnp.float32),
                jnp.zeros((block_rows, kv_heads, group_width, HEAD_SIZE), jnp.float32),
            )
            for number in range(block_count)
        )
    )
    key_rows = lax.all_gather(prompt_keys, "seq", axis=0, tiled=True).reshape(
        -1, kv_heads, HEAD_SIZE
    )
    value_rows = lax.all_gather(prompt_values, "seq", axis=0, tiled=True).reshape(
        -1, kv_heads, HEAD_SIZE
    )
    key_index = jnp.arange(key_rows.shape[0], dtype=jnp.int32)
    key_pos = lookup(offs_all, key_index // tok_rows) * tok_rows + key_index % tok_rows
    lowest = jnp.min(key_pos)
    number = 0
    advance = partial(
        piece_update,
        query_rows=block_q[number],
        query_pos=block_pos[number],
        key_rows=key_rows,
        value_rows=value_rows,
        key_pos=key_pos,
        score_scale=score_scale,
    )
    updated = [lax.cond(lowest > block_top[number], unchanged, advance, start_state[number])]
    states = tuple(updated)
    merged = jnp.concatenate([finish(state) for state in states], axis=0)
    merged = merged.reshape(tok_rows, row_width).astype(jnp.bfloat16)
    dec_rows = appended_queries.shape[0]
    own_count = dec_rows // seq_count
    start_row = seq_index * own_count
    dec_queries = appended_queries.reshape(dec_rows, kv_heads, group_width, HEAD_SIZE)
    own_keys = prompt_keys.reshape(tok_rows, kv_heads, HEAD_SIZE)
    own_values = prompt_values.reshape(tok_rows, kv_heads, HEAD_SIZE)
    own_pos = own_offset * tok_rows + row_ids
    dec_scores = (
        jnp.einsum("rkgd,skd->rkgs", dec_queries, own_keys, preferred_element_type=jnp.float32)
        * score_scale
    )
    visible = (own_pos[None, :] < dec_pos[:, None])[:, None, None, :]
    local_max = jnp.max(jnp.where(visible, dec_scores, masked_score), axis=-1)
    dec_weights = jnp.where(visible, jnp.exp(dec_scores - local_max[..., None]), 0.0)
    local_sum = jnp.sum(dec_weights, axis=-1)
    local_acc = jnp.einsum(
        "rkgs,skd->rkgd",
        dec_weights.astype(jnp.bfloat16),
        own_values,
        preferred_element_type=jnp.float32,
    )
    shared_max = lax.pmax(local_max, "seq")
    factor = jnp.exp(local_max - shared_max)
    part_sum, part_acc = (
        lax.psum_scatter(local_sum * factor, "seq", scatter_dimension=0, tiled=True),
        lax.psum_scatter(local_acc * factor[..., None], "seq", scatter_dimension=0, tiled=True),
    )
    part_max = lax.dynamic_slice_in_dim(shared_max, start_row, own_count, 0)
    mine_q = lax.dynamic_slice_in_dim(dec_queries, start_row, own_count, 0)
    mine_k = lax.dynamic_slice_in_dim(appended_keys, start_row, own_count, 0).reshape(
        own_count, kv_heads, HEAD_SIZE
    )
    mine_v = lax.dynamic_slice_in_dim(appended_values, start_row, own_count, 0).reshape(
        own_count, kv_heads, HEAD_SIZE
    )
    self_score = (
        jnp.einsum("rkgd,rkd->rkg", mine_q, mine_k, preferred_element_type=jnp.float32)
        * score_scale
    )
    final_max = jnp.maximum(part_max, self_score)
    rescale = jnp.exp(part_max - final_max)
    self_weight = jnp.exp(self_score - final_max)
    final_sum = part_sum * rescale + self_weight
    self_term = (
        self_weight.astype(jnp.bfloat16).astype(jnp.float32)[..., None]
        * mine_v.astype(jnp.float32)[:, :, None, :]
    )
    final_acc = part_acc * rescale[..., None] + self_term
    dec_attention = (
        (final_acc / final_sum[..., None]).reshape(own_count, row_width).astype(jnp.bfloat16)
    )
    dec_term = jnp.dot(dec_attention, out_weight, preferred_element_type=jnp.float32)
    dec_out = lax.psum_scatter(dec_term, "head", scatter_dimension=1, tiled=True).astype(
        jnp.bfloat16
    )
    layer_out = lax.psum_scatter(
        jnp.dot(merged, out_weight, preferred_element_type=jnp.float32).astype(jnp.bfloat16),
        "head",
        scatter_dimension=0,
        tiled=True,
    )
    return (layer_out, dec_out)


def solution(mesh):
    in_specs = (
        P("seq", "head"),
        P("seq", "head"),
        P("seq", "head"),
        P("seq"),
        P(None, "head"),
        P(None, "head"),
        P(None, "head"),
        P(),
        P("head", None),
    )
    out_specs = (P(("seq", "head"), None), P("seq", "head"))
    return jax.shard_map(
        on_device, mesh=mesh, in_specs=in_specs, out_specs=out_specs, check_vma=False
    )
```

profile of v0, /device:TPU:0, one launch (start us, length us, event | category | flops | bytes accessed | tf_op | source)
XLA Modules:
  0.0 215.4 jit_solution(10013700093326628951)
XLA Ops:
  8.0 0.9 reshape.144
  8.9 0.7 broadcast_compare_fusion.1
  9.9 23.1 %pmax.7 = f32[8,2,4]{0,2,1:T(4,128)S(1)} all-reduce(f32[8,2,4]{0,2,1:T(4,128)S(1)} %get-tuple-element.39), channel_id=1, replica_groups=mesh['seq'=8,'head'=4] {'seq'}, use_global_device_ids=true, to_apply=%region_9.10 | all-reduce | flops 64 | bytes 512 | tf_op jit(solution)/shard_map/pmax | solution.py:134
  33.2 0.9 reshape.146
  34.5 33.3 %all-reduce.3 = (f32[8,2,4,128]{3,2,1,0:T(4,128)S(1)}, f32[8,2,4]{2,1,0:T(2,128)S(1)}) all-reduce(f32[8,2,4,128]{3,2,1,0:T(4,128)S(1)} %copy.60, f32[8,2,4]{2,1,0:T(2,128)S(1)} %copy.64), channel_id=3, replica_groups=mesh['seq'=8,'head'=4] {'seq'}, use_global_device_ids=true, to_apply=%region_10.11.clone | all-reduce | flops 8256 | bytes 66048
  67.8 1.3 fusion.48
  69.9 0.8 fusion.40
  70.8 0.7 dynamic-slice_convert_fusion
  71.7 0.7 fusion.39
  72.4 8.1 %convolution_bitcast_fusion = f32[4096,1]{1,0:T(8,128)} fusion(bf16[1024,1]{0,1:T(2,128)(2,1)S(1)} %reshape.162, bf16[1024,4096]{1,0:T(8,128)(2,1)} %param.19), kind=kOutput, calls=%fused_computation.19 | convolution fusion | flops 8388608 | bytes 8407040
  80.6 32.3 %all_gather.10 = bf16[1536,256]{1,0:T(8,128)(2,1)S(1)} all-gather(bf16[192,256]{1,0:T(8,128)(2,1)S(1)} %copy-done.2), channel_id=1, replica_groups=mesh['seq'=8,'head'=4] {'seq'}, dimensions={0}, use_global_device_ids=true | all-gather | bytes 884736 | tf_op jit(solution)/shard_map/all_gather | solution.py:90
  112.9 31.6 %all_gather.11 = bf16[1536,256]{1,0:T(8,128)(2,1)S(1)} all-gather(bf16[192,256]{1,0:T(8,128)(2,1)S(1)} %copy-done.3), channel_id=1, replica_groups=mesh['seq'=8,'head'=4] {'seq'}, dimensions={0}, use_global_device_ids=true | all-gather | bytes 884736 | tf_op jit(solution)/shard_map/all_gather | solution.py:93
  144.5 0.7 fusion.42
  145.2 0.8 dynamic-update-slice
  146.0 8.6 %all-reduce = s32[8]{0:T(128)S(1)} all-reduce(s32[8]{0:T(128)S(1)} %dynamic-update-slice), channel_id=1, replica_groups=mesh['seq'=8,'head'=4] {'seq'}, use_global_device_ids=true, to_apply=%add | all-reduce | flops 8 | bytes 64
  156.6 16.5 %conditional.1 = (f32[192,2,4]{0,2,1:T(4,128)S(1)}, f32[192,2,4,128]{3,0,2,1:T(8,128)S(1)}) conditional(s32[]{:T(128)} %convert_element_type.47, (s32[1536]{0:T(1024)S(1)}, s32[192]{0:T(256)S(1)}, bf16[1536,256]{1,0:T(8,128)(2,1)S(1)}, bf16[192,1024]{1,0:T(8,128)(2,1)S(1)}, bf16[1536,256]{1,0:T(8,128)(2,1)S(1)}) %tuple.33, () %tuple.17), branch_computations={%region_3.6_spmd, %region_6.7_spmd} | conditional | flops 1234205184 | bytes 64531288 | solution.py:109
  157.3 5.5 %fusion = (f32[192,2,4]{0,2,1:T(4,128)S(1)}, f32[2,1536,192,4]{1,2,3,0:T(8,128)}) fusion(pred[192,1536]{1,0:T(8,128)(4,1)S(1)} %broadcast_compare_fusion, bf16[192,2,4,128]{3,2,1,0:T(4,128)(2,1)S(1)} %reshape.137, bf16[1536,2,128,1]{2,1,0,3:T(2,128)(2,1)S(1)} %bitcast.62), kind=kOutput, calls=%fused_computation.2 | convolution fusion | flops 611056128 | bytes 10917888 | tf_op jit(solution)/shard_map/cond/branch_0_fun/rkgd,skd->rkgs/dot_general | solution.py:26
  162.9 1.1 reshape.138
  163.9 5.2 %fusion.8 = f32[192,2,4,128]{3,0,2,1:T(8,128)S(1)} fusion(f32[2,1536,192,4]{1,2,3,0:T(8,128)} %get-tuple-element.36, f32[192,2,4]{0,2,1:T(4,128)S(1)} %broadcast_maximum_fusion, pred[192,1536]{1,0:T(8,128)(4,1)S(1)} %broadcast_compare_fusion, bf16[1536,2,128,1]{2,1,0,3:T(2,128)(2,1)} %bitcast.63), kind=kOutput, calls=%fused_computation.9 | convolution fusion | flops 613416960 | bytes 11311104 | tf_op jit(solution)/shard_map/cond/branch_0_fun/rkgs,skd->rkgd/dot_general | solution.py:34
  169.2 1.2 slice-done.2
  170.4 2.6 %fusion.4 = f32[192,2,4]{0,2,1:T(4,128)S(1)} fusion(f32[2,1536,192,4]{1,2,3,0:T(8,128)S(1)} %bitcast.61, f32[192,2,4]{0,2,1:T(4,128)S(1)} %broadcast_maximum_fusion, pred[192,1536]{1,0:T(8,128)(4,1)S(1)} %broadcast_compare_fusion), kind=kLoop, calls=%fused_computation.6 | loop fusion | flops 9435648 | bytes 9744384 | tf_op jit(solution)/shard_map/cond/branch_0_fun/reduce_sum | solution.py:33
  174.0 6.3 %convolution_convert_fusion = bf16[192,4096]{1,0:T(8,128)(2,1)} fusion(bf16[192,1024]{1,0:T(8,128)(2,1)S(1)} %convert_element_type.49, bf16[1024,4096]{1,0:T(8,128)(2,1)} %param.19), kind=kOutput, calls=%fused_computation.18 | convolution fusion | flops 1611399168 | bytes 10354688 | tf_op jit(solution)/shard_map/dot_general | solution.py:169
  180.4 1.8 copy.81
  182.3 26.3 %reduce-scatter.5.cloned.1.call-done = bf16[48,4096]{1,0:T(8,128)(2,1)} async-done(((bf16[192,4096]{1,0:T(8,128)(2,1)}), bf16[48,4096]{1,0:T(8,128)(2,1)}) %reduce-scatter.5.cloned.1.call-update) | async-done | bytes 393232 | tf_op jit(solution)/shard_map/reduce_scatter | solution.py:168
  (44 shorter events, 4.3 us)
Async XLA Ops:
  7.2 2.5 %copy-start = (bf16[8,1024]{1,0:T(8,128)(2,1)S(1)}, bf16[8,1024]{1,0:T(8,128)(2,1)}, u32[]{:S(2)}) copy-start(bf16[8,1024]{1,0:T(8,128)(2,1)} %param.15) | copy-start | bytes 49156
  7.2 73.4 %copy-start.2 = (bf16[192,256]{1,0:T(8,128)(2,1)S(1)}, bf16[192,256]{1,0:T(8,128)(2,1)}, u32[]{:S(2)}) copy-start(bf16[192,256]{1,0:T(8,128)(2,1)} %param.12) | copy-start | bytes 294916
  7.2 105.7 %copy-start.3 = (bf16[192,256]{1,0:T(8,128)(2,1)S(1)}, bf16[192,256]{1,0:T(8,128)(2,1)}, u32[]{:S(2)}) copy-start(bf16[192,256]{1,0:T(8,128)(2,1)} %param.13) | copy-start | bytes 294916
  7.2 149.4 %copy-start.1 = (bf16[192,1024]{1,0:T(8,128)(2,1)S(1)}, bf16[192,1024]{1,0:T(8,128)(2,1)}, u32[]{:S(2)}) copy-start(bf16[192,1024]{1,0:T(8,128)(2,1)} %param.11) | copy-start | bytes 1179652
  7.2 173.2 %reduce-scatter.7.cloned.1.call-start = ((), (), s32[]{:S(2)}) async-start(), calls=%async_computation.3 | async-start | bytes 2621440
  80.5 128.0 %reduce-scatter.5.cloned.1.call-start = ((), (), s32[]{:S(2)}) async-start(), calls=%async_computation.2 | async-start | bytes 1966080 | tf_op jit(solution)/shard_map/reduce_scatter | solution.py:168
  162.8 6.2 %slice-start = ((s8[9437184]{0:T(1024)(128)(4,1)}), s8[1048576]{0:T(1024)(128)(4,1)S(1)}, s32[]{:S(2)}) async-start(s8[9437184]{0:T(1024)(128)(4,1)} %bitcast.60), calls=%async_computation.4 | async-start | bytes 2097152 | tf_op jit(solution)/shard_map/cond
  163.9 5.3 %slice-start.1 = ((s8[9437184]{0:T(1024)(128)(4,1)}), s8[4194304]{0:T(1024)(128)(4,1)S(1)}, s32[]{:S(2)}) async-start(s8[9437184]{0:T(1024)(128)(4,1)} %bitcast.60), calls=%async_computation.5 | async-start | bytes 8388608 | tf_op jit(solution)/shard_map/cond
  163.9 6.5 %slice-start.2 = ((s8[9437184]{0:T(1024)(128)(4,1)}), s8[4194304]{0:T(1024)(128)(4,1)S(1)}, s32[]{:S(2)}) async-start(s8[9437184]{0:T(1024)(128)(4,1)} %bitcast.60), calls=%async_computation.6 | async-start | bytes 8388608 | tf_op jit(solution)/shard_map/cond
Sparse Core Ops, SparseCore 0:
  80.6 29.9 reduce-scatter.6
  180.5 27.9 reduce-scatter.4
where the time goes:
time: 216 us; the launch traced here: 215 us
  blocking collectives  129 us (60%)
  matrix products  26.3 us (12%)
  waiting for transfers between devices  26.3 us (12%)
  between operations  16.2 us (8%)
  local copies, waits for them, and re-layouts  10.2 us (5%)
  other arithmetic  7.03 us (3%)
    unnamed x2, blocking collectives  41.9 us
    all_gather x1, blocking collectives, on_device(): lax.all_gather(prompt_keys, 'seq', axis=0, tiled=True)  32.3 us
    all_gather x1, blocking collectives, on_device(): lax.all_gather(prompt_values, 'seq', axis=0, tiled=True)  31.6 us
    reduce_scatter x1, waiting for transfers between devices, on_device(): lax.psum_scatter(jnp.dot(merged, out_weight, preferred_element_type=jnp.f...  26.3 us
    pmax x1, blocking collectives, on_device(): shared_max = lax.pmax(local_max, 'seq')  23.1 us
    unnamed x1, matrix products  8.06 us
    dot_general x1, matrix products, on_device(): jnp.dot(merged, out_weight, preferred_element_type=jnp.float32)  6.34 us
    dot_general x1, matrix products, piece_update(): jnp.einsum('rkgd,skd->rkgs', query_rows, key_rows, preferred_element_type...  5.5 us
  transfers between devices with their start and end apart: 2, of which 1 were waited for; matrix products, arithmetic and copies ran while one was open for 12% of the time, Pallas kernels for 0%

commit v1 on v0

v1 whole, which is shorter than its diff:
```python
import functools
import math

import jax
import jax.numpy as jnp
from jax import lax
from jax.experimental import pallas as pl
from jax.experimental.pallas import tpu as pltpu
from jax.sharding import PartitionSpec as P

QUERY_HEADS = 32
KEY_VALUE_HEADS = 8
HEAD_SIZE = 128
GROUP = QUERY_HEADS // KEY_VALUE_HEADS
MESH = pl.DeviceIdType.MESH

masked_score = -1e30
exp2_scale = HEAD_SIZE ** (-0.5) * math.log2(math.e)


def tiled(column, width):
    return jnp.concatenate([column] * (width // column.shape[1]), axis=1)


def softmax_step(scores, allowed, value_rows, m_ref, l_ref, acc_ref, slot):
    scores = jnp.where(allowed, scores, masked_score)
    old_max = m_ref[slot]
    new_max = jnp.maximum(old_max, jnp.max(scores, axis=1, keepdims=True))
    weights = jnp.exp2((scores - tiled(new_max, scores.shape[1])) * exp2_scale)
    factor = jnp.exp2((old_max - new_max) * exp2_scale)
    m_ref[slot] = new_max
    l_ref[slot] = l_ref[slot] * factor + jnp.sum(weights, axis=1, keepdims=True)
    added = jnp.dot(
        weights.astype(jnp.bfloat16), value_rows, preferred_element_type=jnp.float32
    )
    acc_ref[slot] = acc_ref[slot] * factor + added


def kernel(
    n_seq, own_dec, chunk,
    q_ref, k_ref, v_ref, span_ref, aq_ref, ak_ref, av_ref, pos_ref, w_hbm,
    out_ref, dec_ref,
    kbuf, vbuf, obuf, wbuf, m_ref, l_ref, acc_ref, md_ref, ld_ref, accd_ref,
    attn, pbuf, own, send1, recv1, send2, recv2, dpart, dsend, drecv,
    local_sem, w_sem, ss, rs, ss1, rs1, ss2, rs2, dss, drs,
):
    tok, width = q_ref.shape
    kv_heads = k_ref.shape[1] // HEAD_SIZE
    n_dec = aq_ref.shape[0]
    model = w_hbm.shape[1]
    part = tok // 4
    line = n_seq // 2
    seq = lax.axis_index("seq")
    head = lax.axis_index("head")
    z, x = seq // 2, seq % 2
    y, c = head // 2, head % 2
    to_x = (2 * z + 1 - x, head)
    to_right = (jnp.minimum(seq + 2, n_seq - 1), head)
    to_left = (jnp.maximum(seq - 2, 0), head)
    to_core = (seq, 2 * y + 1 - c)
    to_y = (seq, 2 * (1 - y) + c)
    to_diag = (seq, 2 * (1 - y) + 1 - c)
    has_left, has_right = z > 0, z < line - 1

    weight_copy = pltpu.make_async_copy(w_hbm, wbuf, w_sem)
    weight_copy.start()
    sources = (span_ref, k_ref, v_ref)
    buffers = (obuf, kbuf, vbuf)
    locals_ = [
        pltpu.make_async_copy(sources[i], buffers[i].at[seq], local_sem.at[i]) for i in range(3)
    ]
    for copy in locals_:
        copy.start()

    barrier = pltpu.get_barrier_semaphore()
    for peer in (to_x, to_core, to_y, to_diag):
        pl.semaphore_signal(barrier, inc=1, device_id=peer, device_id_type=MESH)
    pl.when(has_left)(
        lambda: pl.semaphore_signal(barrier, inc=1, device_id=to_left, device_id_type=MESH)
    )
    pl.when(has_right)(
        lambda: pl.semaphore_signal(barrier, inc=1, device_id=to_right, device_id_type=MESH)
    )
    pl.semaphore_wait(barrier, 4 + jnp.where(has_left, 1, 0) + jnp.where(has_right, 1, 0))

    targets = (to_left, to_right, to_x)

    def moved(piece, origin, way, first=False):
        slot = buffers[piece].at[origin]
        return pltpu.make_async_remote_copy(
            src_ref=sources[piece] if first else slot,
            dst_ref=slot,
            send_sem=ss.at[way, piece, origin],
            recv_sem=rs.at[piece, origin],
            device_id=targets[way],
            device_id_type=MESH,
        )

    def nearest(j):
        reach = jnp.minimum(z, line - 1 - z)
        half = (j + 1) // 2
        both = jnp.where(j % 2 == 1, z - half, z + half)
        single = jnp.where(z < line - 1 - z, z + (j - reach), z - (j - reach))
        return jnp.where(j <= 2 * reach, both, single)

    for piece in range(3):
        pl.when(has_left)(lambda: moved(piece, seq, 0, True).start())
        pl.when(has_right)(lambda: moved(piece, seq, 1, True).start())
        moved(piece, seq, 2, True).start()

    def dec_rows(ref, h, g=0):
        col = (h * GROUP + g) * HEAD_SIZE if ref is aq_ref else h * HEAD_SIZE
        return ref[:, col : col + HEAD_SIZE].astype(jnp.float32)

    for h in range(kv_heads):
        q32 = jnp.concatenate([dec_rows(aq_ref, h, g) for g in range(GROUP)], axis=0)
        k32 = jnp.concatenate([dec_rows(ak_ref, h)] * GROUP, axis=0)
        v32 = jnp.concatenate([dec_rows(av_ref, h)] * GROUP, axis=0)
        self_score = jnp.sum(q32 * k32, axis=1, keepdims=True)
        md_ref[h] = jnp.broadcast_to(self_score, q32.shape)
        ld_ref[h] = jnp.ones(q32.shape, jnp.float32)
        accd_ref[h] = v32
    m_ref[...] = jnp.full(m_ref.shape, masked_score, jnp.float32)
    l_ref[...] = jnp.zeros(l_ref.shape, jnp.float32)
    acc_ref[...] = jnp.zeros(acc_ref.shape, jnp.float32)
    own_off = span_ref[0:1, 0:1]
    dec_index = lax.broadcasted_iota(jnp.int32, (GROUP * n_dec, 1), 0) % n_dec
    dec_limit = jnp.zeros((GROUP * n_dec, 1), jnp.int32)
    for i in range(n_dec):
        dec_limit = jnp.where(dec_index == i, pos_ref[i], dec_limit)
    for copy in locals_:
        copy.wait()

    def pair_step(j, carry):
        @pl.when(j + 1 < line)
        def _():
            zz = nearest(j + 1)
            origin = 2 * zz + x
            for piece in range(3):
                moved(piece, origin, 2).wait_recv()
                pl.when((zz < z) & has_right)(lambda: moved(piece, origin, 1).start())
                pl.when((zz > z) & has_left)(lambda: moved(piece, origin, 0).start())
                moved(piece, origin, 2).start()

        zz = nearest(j)
        for piece in range(3):
            moved(piece, 2 * zz + 1 - x, 2).wait_recv()
        key_id = lax.broadcasted_iota(jnp.int32, (1, 2 * tok), 1)
        first = key_id < tok
        offset = jnp.where(first, obuf[2 * zz][0:1, 0:1], obuf[2 * zz + 1][0:1, 0:1])
        key_pos = offset * tok + jnp.where(first, key_id, key_id - tok)
        query_pos = own_off * tok + lax.broadcasted_iota(jnp.int32, (tok, 1), 0)
        allowed = key_pos <= query_pos
        dec_allowed = key_pos < dec_limit
        for h in range(kv_heads):
            cols = slice(h * HEAD_SIZE, (h + 1) * HEAD_SIZE)
            keys = jnp.concatenate([kbuf[2 * zz, :, cols], kbuf[2 * zz + 1, :, cols]], axis=0)
            vals = jnp.concatenate([vbuf[2 * zz, :, cols], vbuf[2 * zz + 1, :, cols]], axis=0)
            for g in range(GROUP):
                i = h * GROUP + g
                queries = q_ref[:, i * HEAD_SIZE : (i + 1) * HEAD_SIZE]
                scores = lax.dot_general(
                    queries, keys, (((1,), (1,)), ((), ())),
                    preferred_element_type=jnp.float32,
                )
                softmax_step(scores, allowed, vals, m_ref, l_ref, acc_ref, i)
            q32 = jnp.concatenate([dec_rows(aq_ref, h, g) for g in range(GROUP)], axis=0)
            scores = lax.dot_general(
                q32.astype(jnp.bfloat16), keys, (((1,), (1,)), ((), ())),
                preferred_element_type=jnp.float32,
            )
            softmax_step(scores, dec_allowed, vals, md_ref, ld_ref, accd_ref, h)
        return carry

    lax.fori_loop(0, line, pair_step, 0)

    pad = attn.shape[0] - tok - n_dec
    for h in range(kv_heads):
        dec = accd_ref[h] / ld_ref[h]
        for g in range(GROUP):
            i = h * GROUP + g
            cols = slice(i * HEAD_SIZE, (i + 1) * HEAD_SIZE)
            attn[0:tok, cols] = (acc_ref[i] / l_ref[i]).astype(jnp.bfloat16)
            rows = dec[g * n_dec : (g + 1) * n_dec]
            if pad:
                rows = jnp.concatenate([rows, jnp.zeros((pad, HEAD_SIZE), jnp.float32)], axis=0)
            attn[tok:, cols] = rows.astype(jnp.bfloat16)
    weight_copy.wait()

    n_chunk = model // chunk

    def core_copy(i):
        return pltpu.make_async_remote_copy(
            src_ref=send1.at[i], dst_ref=recv1.at[i], send_sem=ss1.at[i], recv_sem=rs1.at[i],
            device_id=to_core, device_id_type=MESH,
        )

    def y_copy(i):
        return pltpu.make_async_remote_copy(
            src_ref=send2.at[i], dst_ref=recv2.at[i], send_sem=ss2.at[i], recv_sem=rs2.at[i],
            device_id=to_y, device_id_type=MESH,
        )

    def block(index):
        return pl.ds(pl.multiple_of(index * part, 8), part)

    def project(i, carry):
        @pl.when(i < n_chunk)
        def _():
            cols = pl.ds(pl.multiple_of(i * chunk, chunk), chunk)
            pbuf[...] = jnp.dot(attn[...], wbuf[:, cols], preferred_element_type=jnp.float32)
            send1[i, 0:part] = pbuf[block(2 * (1 - y) + 1 - c)].astype(jnp.bfloat16)
            send1[i, part:] = pbuf[block(2 * y + 1 - c)].astype(jnp.bfloat16)
            core_copy(i).start()
            own[i, 0:part] = pbuf[block(2 * (1 - y) + c)]
            own[i, part:] = pbuf[block(2 * y + c)]
            dpart[:, cols] = pbuf[tok : tok + n_dec]

        @pl.when(i > 0)
        def _():
            core_copy(i - 1).wait_recv()
            total = own[i - 1, 0:part] + recv1[i - 1, 0:part].astype(jnp.float32)
            send2[i - 1] = total.astype(jnp.bfloat16)
            y_copy(i - 1).start()

        return carry

    lax.fori_loop(0, n_chunk + 1, project, 0)

    quarter = model // 4
    mine = pl.ds(seq * own_dec, own_dec)

    def dec_copy(way, peer):
        return pltpu.make_async_remote_copy(
            src_ref=dsend.at[way], dst_ref=drecv.at[way],
            send_sem=dss.at[way], recv_sem=drs.at[way],
            device_id=peer, device_id_type=MESH,
        )

    dec_copies = []
    for way, peer in enumerate((to_core, to_y, to_diag)):
        cols = pl.ds(pl.multiple_of(peer[1] * quarter, 128), quarter)
        dsend[way] = dpart[mine, cols]
        dec_copies.append(dec_copy(way, peer))
        dec_copies[-1].start()

    def gather_sum(i, carry):
        y_copy(i).wait_recv()
        cols = pl.ds(pl.multiple_of(i * chunk, chunk), chunk)
        total = own[i, part:] + recv1[i, part:].astype(jnp.float32)
        out_ref[:, cols] = (total + recv2[i].astype(jnp.float32)).astype(jnp.bfloat16)
        y_copy(i).wait_send()
        core_copy(i).wait_send()
        return carry

    lax.fori_loop(0, n_chunk, gather_sum, 0)
    for copy in dec_copies:
        copy.wait()
    dec_total = dpart[mine, pl.ds(pl.multiple_of(head * quarter, 128), quarter)]
    dec_ref[...] = (dec_total + drecv[0] + drecv[1] + drecv[2]).astype(jnp.bfloat16)

    def drain(j, carry):
        zz = nearest(j)
        origin = 2 * zz + x
        for piece in range(3):
            pl.when((zz <= z) & has_right)(lambda: moved(piece, origin, 1).wait_send())
            pl.when((zz >= z) & has_left)(lambda: moved(piece, origin, 0).wait_send())
            moved(piece, origin, 2).wait_send()
        return carry

    lax.fori_loop(0, line, drain, 0)


def on_device(
    prompt_queries, prompt_keys, prompt_values, span_offset,
    appended_queries, appended_keys, appended_values, dec_pos, out_weight,
):
    n_seq = lax.axis_size("seq")
    tok, width = prompt_queries.shape
    kv_width = prompt_keys.shape[1]
    kv_heads = kv_width // HEAD_SIZE
    heads = kv_heads * GROUP
    n_dec = appended_queries.shape[0]
    own_dec = n_dec // n_seq
    model = out_weight.shape[1]
    chunk = 512
    n_chunk = model // chunk
    part = tok // 4
    rows = tok + -(-n_dec // 16) * 16
    span = jnp.broadcast_to(span_offset, (8, 128))
    vmem = pl.BlockSpec(memory_space=pltpu.VMEM)
    f32, b16 = jnp.float32, jnp.bfloat16
    dma = pltpu.SemaphoreType.DMA
    return pl.pallas_call(
        functools.partial(kernel, n_seq, own_dec, chunk),
        out_shape=(
            jax.ShapeDtypeStruct((part, model), b16),
            jax.ShapeDtypeStruct((own_dec, model // 4), b16),
        ),
        in_specs=[vmem] * 7
        + [pl.BlockSpec(memory_space=pltpu.SMEM), pl.BlockSpec(memory_space=pl.ANY)],
        out_specs=(vmem, vmem),
        scratch_shapes=[
            pltpu.VMEM((n_seq, tok, kv_width), b16),
            pltpu.VMEM((n_seq, tok, kv_width), b16),
            pltpu.VMEM((n_seq, 8, 128), jnp.int32),
            pltpu.VMEM(out_weight.shape, b16),
            pltpu.VMEM((heads, tok, HEAD_SIZE), f32),
            pltpu.VMEM((heads, tok, HEAD_SIZE), f32),
            pltpu.VMEM((heads, tok, HEAD_SIZE), f32),
            pltpu.VMEM((kv_heads, GROUP * n_dec, HEAD_SIZE), f32),
            pltpu.VMEM((kv_heads, GROUP * n_dec, HEAD_SIZE), f32),
            pltpu.VMEM((kv_heads, GROUP * n_dec, HEAD_SIZE), f32),
            pltpu.VMEM((rows, width), b16),
            pltpu.VMEM((rows, chunk), f32),
            pltpu.VMEM((n_chunk, 2 * part, chunk), f32),
            pltpu.VMEM((n_chunk, 2 * part, chunk), b16),
            pltpu.VMEM((n_chunk, 2 * part, chunk), b16),
            pltpu.VMEM((n_chunk, part, chunk), b16),
            pltpu.VMEM((n_chunk, part, chunk), b16),
            pltpu.VMEM((n_dec, model), f32),
            pltpu.VMEM((3, own_dec, model // 4), f32),
            pltpu.VMEM((3, own_dec, model // 4), f32),
            dma((3,)), dma,
            dma((3, 3, n_seq)), dma((3, n_seq)),
            dma((n_chunk,)), dma((n_chunk,)), dma((n_chunk,)), dma((n_chunk,)),
            dma((3,)), dma((3,)),
        ],
        compiler_params=pltpu.CompilerParams(
            collective_id=0, has_side_effects=True, vmem_limit_bytes=60 * 2**20
        ),
    )(
        prompt_queries, prompt_keys, prompt_values, span,
        appended_queries, appended_keys, appended_values, dec_pos, out_weight,
    )


def solution(mesh):
    in_specs = (
        P("seq", "head"),
        P("seq", "head"),
        P("seq", "head"),
        P("seq"),
        P(None, "head"),
        P(None, "head"),
        P(None, "head"),
        P(),
        P("head", None),
    )
    out_specs = (P(("seq", "head"), None), P("seq", "head"))
    return jax.shard_map(
        on_device, mesh=mesh, in_specs=in_specs, out_specs=out_specs, check_vma=False
    )
```

time: 216 us -> 50.5 us (0.23)
  blocking collectives: 129 us -> 0 us
  Pallas kernels: 0 us -> 45.3 us
  matrix products: 26.3 us -> 0 us
  waiting for transfers between devices: 26.3 us -> 0 us
  between operations: 16.2 us -> 1.28 us
  other arithmetic: 7.03 us -> 0 us
  local copies, waits for them, and re-layouts: 10.2 us -> 3.63 us
    all_gather x2 -> x0, blocking collectives: 63.9 us -> none  [the longest x1 32.3 us: on_device(): lax.all_gather(prompt_keys, 'seq', axis=0, tiled=True)]
    pallas_call x0 -> x1, Pallas kernels: none -> 45.3 us  [on_device(): pl.pallas_call(functools.partial(kernel, n_seq, own_dec, chunk), out_shap...]
    unnamed x2 -> x0, blocking collectives: 41.9 us -> none
    reduce_scatter x1 -> x0, waiting for transfers between devices: 26.3 us -> none  [on_device(): lax.psum_scatter(jnp.dot(merged, out_weight, preferred_element_type=jnp.f...]
    pmax x1 -> x0, blocking collectives: 23.1 us -> none  [on_device(): shared_max = lax.pmax(local_max, 'seq')]
    dot_general x6 -> x0, matrix products: 18.3 us -> none  [the longest x1 6.34 us: on_device(): jnp.dot(merged, out_weight, preferred_element_type=jnp.float32)]
    unnamed x1 -> x0, matrix products: 8.06 us -> none
    reshape x5 -> x0, local copies, waits for them, and re-layouts: 3.36 us -> none  [the longest x1 1.06 us: on_device(): lax.all_gather(prompt_values, 'seq', axis=0, tiled=True)]
  transfers between devices with their start and end apart: 2 -> 0, of which waited for: 1 -> 0; matrix products, arithmetic and copies ran while one was open for 12% -> 0% of each run, Pallas kernels for 0% -> 0%
where the time goes in v1:
time: 50.5 us; the launch traced here: 50.3 us
  Pallas kernels  45.3 us (90%)
  local copies, waits for them, and re-layouts  3.63 us (7%)
  between operations  1.28 us (3%)
    pallas_call x1, Pallas kernels, on_device(): pl.pallas_call(functools.partial(kernel, n_seq, own_dec, chunk), out_shap...  45.3 us
    unnamed x2, local copies, waits for them, and re-layouts  3.03 us

profile of v1, /device:TPU:0, one launch (start us, length us, event | category | flops | bytes accessed | tf_op | source)
XLA Modules:
  0.0 50.3 jit_solution(2910073704258858205)
XLA Ops:
  1.3 0.6 %broadcast_in_dim.2.span_ref = s32[8,128]{1,0:T(8,128)} broadcast(s32[]{:T(128)} %bitcast.1), dimensions={} | broadcast | bytes 4100 | tf_op jit(solution)/shard_map/broadcast_in_dim | solution.py:290
  1.9 45.3 %shard_map.107 = (bf16[48,4096]{1,0:T(8,128)(2,1)}, bf16[1,1024]{1,0:T(2,128)(2,1)}) custom-call(bf16[192,1024]{1,0:T(8,128)(2,1)} %q_ref.1, bf16[192,256]{1,0:T(8,128)(2,1)} %k_ref.1, bf16[192,256]{1,0:T(8,128)(2,1)} %v_ref.1, s32[8,128]{1,0:T(8,128)} %broadcast_in_dim.2.span_ref, bf16[8,1024]{1,0:T(8,128)(2,1)} %aq_ref.1, bf16[8,256]{1,0:T(8,128)(2,1)} %ak_ref.1, ...), custom_call_target="tpu_custom_call" | custom-call | tf_op jit(solution)/shard_map/pallas_call | solution.py:294
  47.2 1.8 %copy.14 = bf16[48,4096]{1,0:T(8,128)(2,1)} copy(bf16[48,4096]{1,0:T(8,128)(2,1)} %get-tuple-element.4) | data formatting | bytes 786432
  49.0 1.3 %copy.15 = bf16[1,1024]{1,0:T(2,128)(2,1)} copy(bf16[1,1024]{1,0:T(2,128)(2,1)} %get-tuple-element.5) | data formatting | bytes 4096

commit v2 on v1

--- a/solution.py
+++ b/solution.py
@@ -34,6 +34,17 @@
         weights.astype(jnp.bfloat16), value_rows, preferred_element_type=jnp.float32
     )
     acc_ref[slot] = acc_ref[slot] * factor + added
+
+
+def hand_on(layer_in, dec_in, layer_out, dec_out):
+    layer_out[...] = layer_in[...]
+    dec_out[...] = dec_in[...]
+
+
+def row_cuts(tok):
+    first = max(tok // 96, 1) * 16
+    half = (tok - first) // 32 * 16
+    return ((0, first), (first, half), (first + half, tok - first - half))
 
 
 def kernel(
@@ -64,10 +75,16 @@
 
     weight_copy = pltpu.make_async_copy(w_hbm, wbuf, w_sem)
     weight_copy.start()
-    sources = (span_ref, k_ref, v_ref)
-    buffers = (obuf, kbuf, vbuf)
+    cuts = row_cuts(tok)
+    pieces = [(k_ref, kbuf, cuts[0]), (v_ref, vbuf, cuts[0]), (span_ref, obuf, (0, 8))]
+    pieces += [(k_ref, kbuf, cut) for cut in cuts[1:]]
+    pieces += [(v_ref, vbuf, cut) for cut in cuts[1:]]
+    early, late = (), tuple(range(len(pieces)))
     locals_ = [
-        pltpu.make_async_copy(sources[i], buffers[i].at[seq], local_sem.at[i]) for i in range(3)
+        pltpu.make_async_copy(source, buffer.at[seq], local_sem.at[i])
+        for i, (source, buffer) in enumerate(
+            ((span_ref, obuf), (k_ref, kbuf), (v_ref, vbuf))
+        )
     ]
     for copy in locals_:
         copy.start()
@@ -86,9 +103,10 @@
     targets = (to_left, to_right, to_x)
 
     def moved(piece, origin, way, first=False):
-        slot = buffers[piece].at[origin]
+        source, buffer, (begin, size) = pieces[piece]
+        slot = buffer.at[origin, pl.ds(begin, size)]
         return pltpu.make_async_remote_copy(
-            src_ref=sources[piece] if first else slot,
+            src_ref=source.at[pl.ds(begin, size)] if first else slot,
             dst_ref=slot,
             send_sem=ss.at[way, piece, origin],
             recv_sem=rs.at[piece, origin],
@@ -103,10 +121,11 @@
         single = jnp.where(z < line - 1 - z, z + (j - reach), z - (j - reach))
         return jnp.where(j <= 2 * reach, both, single)
 
-    for piece in range(3):
+    partner = 2 * z + 1 - x
+    for piece in early + late:
+        moved(piece, seq, 2, True).start()
         pl.when(has_left)(lambda: moved(piece, seq, 0, True).start())
         pl.when(has_right)(lambda: moved(piece, seq, 1, True).start())
-        moved(piece, seq, 2, True).start()
 
     def dec_rows(ref, h, g=0):
         col = (h * GROUP + g) * HEAD_SIZE if ref is aq_ref else h * HEAD_SIZE
@@ -131,19 +150,37 @@
     for copy in locals_:
         copy.wait()
 
+    for piece in early:
+        moved(piece, partner, 2).wait_recv()
+        pl.when(has_left)(lambda: moved(piece, partner, 0).start())
+        pl.when(has_right)(lambda: moved(piece, partner, 1).start())
+
+    arrivals = [(piece, False) for piece in early + late] + [(piece, True) for piece in early]
+
+    def relay(distance):
+        for piece, other in arrivals:
+            column = 1 - x if other else x
+
+            @pl.when(z >= distance)
+            def _():
+                origin = 2 * (z - distance) + column
+                moved(piece, origin, 1).wait_recv()
+                pl.when(has_right)(lambda: moved(piece, origin, 1).start())
+                if piece in late:
+                    moved(piece, origin, 2).start()
+
+            @pl.when(z + distance < line)
+            def _():
+                origin = 2 * (z + distance) + column
+                moved(piece, origin, 0).wait_recv()
+                pl.when(has_left)(lambda: moved(piece, origin, 0).start())
+                if piece in late:
+                    moved(piece, origin, 2).start()
+
     def pair_step(j, carry):
-        @pl.when(j + 1 < line)
-        def _():
-            zz = nearest(j + 1)
-            origin = 2 * zz + x
-            for piece in range(3):
-                moved(piece, origin, 2).wait_recv()
-                pl.when((zz < z) & has_right)(lambda: moved(piece, origin, 1).start())
-                pl.when((zz > z) & has_left)(lambda: moved(piece, origin, 0).start())
-                moved(piece, origin, 2).start()
-
+        pl.when(j + 1 < line)(lambda: relay(j + 1))
         zz = nearest(j)
-        for piece in range(3):
+        for piece in late:
             moved(piece, 2 * zz + 1 - x, 2).wait_recv()
         key_id = lax.broadcasted_iota(jnp.int32, (1, 2 * tok), 1)
         first = key_id < tok
@@ -259,15 +296,17 @@
     dec_total = dpart[mine, pl.ds(pl.multiple_of(head * quarter, 128), quarter)]
     dec_ref[...] = (dec_total + drecv[0] + drecv[1] + drecv[2]).astype(jnp.bfloat16)
 
-    def drain(j, carry):
-        zz = nearest(j)
-        origin = 2 * zz + x
-        for piece in range(3):
+    def drain(zz, carry):
+        for piece, other in arrivals:
+            origin = 2 * zz + (1 - x if other else x)
             pl.when((zz <= z) & has_right)(lambda: moved(piece, origin, 1).wait_send())
             pl.when((zz >= z) & has_left)(lambda: moved(piece, origin, 0).wait_send())
-            moved(piece, origin, 2).wait_send()
+            if piece in late:
+                moved(piece, origin, 2).wait_send()
         return carry
 
+    for piece in early:
+        moved(piece, seq, 2).wait_send()
     lax.fori_loop(0, line, drain, 0)
 
 
@@ -291,7 +330,7 @@
     vmem = pl.BlockSpec(memory_space=pltpu.VMEM)
     f32, b16 = jnp.float32, jnp.bfloat16
     dma = pltpu.SemaphoreType.DMA
-    return pl.pallas_call(
+    results = pl.pallas_call(
         functools.partial(kernel, n_seq, own_dec, chunk),
         out_shape=(
             jax.ShapeDtypeStruct((part, model), b16),
@@ -322,7 +361,7 @@
             pltpu.VMEM((3, own_dec, model // 4), f32),
             pltpu.VMEM((3, own_dec, model // 4), f32),
             dma((3,)), dma,
-            dma((3, 3, n_seq)), dma((3, n_seq)),
+            dma((3, 7, n_seq)), dma((7, n_seq)),
             dma((n_chunk,)), dma((n_chunk,)), dma((n_chunk,)), dma((n_chunk,)),
             dma((3,)), dma((3,)),
         ],
@@ -333,6 +372,13 @@
         prompt_queries, prompt_keys, prompt_values, span,
         appended_queries, appended_keys, appended_values, dec_pos, out_weight,
     )
+    return pl.pallas_call(
+        hand_on,
+        out_shape=tuple(jax.ShapeDtypeStruct(r.shape, r.dtype) for r in results),
+        in_specs=[vmem] * 2,
+        out_specs=(vmem, vmem),
+        compiler_params=pltpu.CompilerParams(vmem_limit_bytes=4 * 2**20),
+    )(*results)
 
 
 def solution(mesh):

time: 50.5 us -> 47.6 us (0.943)
  Pallas kernels: 45.3 us -> 43.8 us
  local copies, waits for them, and re-layouts: 3.63 us -> 2.27 us
    pallas_call x1, Pallas kernels: 45.3 us -> 43 us  [on_device(): pl.pallas_call(functools.partial(kernel, n_seq, own_dec, chunk), out_shap...]
    unnamed x2 -> x4, local copies, waits for them, and re-layouts: 3.03 us -> 1.67 us
    pallas_call x0 -> x1, Pallas kernels: none -> 0.77 us  [on_device(): pl.pallas_call(hand_on, out_shape=tuple((jax.ShapeDtypeStruct(r.shape, r....]
where the time goes in v2:
time: 47.6 us; the launch traced here: 47.4 us
  Pallas kernels  43.8 us (92%)
  local copies, waits for them, and re-layouts  2.27 us (5%)
  between operations  1.29 us (3%)
    pallas_call x1, Pallas kernels, on_device(): pl.pallas_call(functools.partial(kernel, n_seq, own_dec, chunk), out_shap...  43 us
    unnamed x4, local copies, waits for them, and re-layouts  1.67 us

profile of v2, /device:TPU:0, one launch (start us, length us, event | category | flops | bytes accessed | tf_op | source)
XLA Modules:
  0.0 47.4 jit_solution(4311747969001272148)
XLA Ops:
  1.3 0.6 %broadcast_in_dim.2.span_ref = s32[8,128]{1,0:T(8,128)} broadcast(s32[]{:T(128)} %bitcast.1), dimensions={} | broadcast | bytes 4100 | tf_op jit(solution)/shard_map/broadcast_in_dim | solution.py:329
  1.9 43.0 %shard_map.107 = (bf16[48,4096]{1,0:T(8,128)(2,1)}, bf16[1,1024]{1,0:T(2,128)(2,1)}) custom-call(bf16[192,1024]{1,0:T(8,128)(2,1)} %q_ref.1, bf16[192,256]{1,0:T(8,128)(2,1)} %k_ref.1, bf16[192,256]{1,0:T(8,128)(2,1)} %v_ref.1, s32[8,128]{1,0:T(8,128)} %broadcast_in_dim.2.span_ref, bf16[8,1024]{1,0:T(8,128)(2,1)} %aq_ref.1, bf16[8,256]{1,0:T(8,128)(2,1)} %ak_ref.1, ...), custom_call_target="tpu_custom_call" | custom-call | tf_op jit(solution)/shard_map/pallas_call | solution.py:333
  44.9 0.0 copy-start
  44.9 1.0 %copy-done = bf16[48,4096]{1,0:T(8,128)(2,1)S(1)} copy-done((bf16[48,4096]{1,0:T(8,128)(2,1)S(1)}, bf16[48,4096]{1,0:T(8,128)(2,1)}, u32[]{:S(2)}) %copy-start) | copy-done | bytes 393240
  45.9 0.0 copy-start.1
  45.9 0.7 %copy-done.1 = bf16[1,1024]{1,0:T(2,128)(2,1)S(1)} copy-done((bf16[1,1024]{1,0:T(2,128)(2,1)S(1)}, bf16[1,1024]{1,0:T(2,128)(2,1)}, u32[]{:S(2)}) %copy-start.1) | copy-done | bytes 2072
  46.6 0.8 %shard_map.108 = (bf16[48,4096]{1,0:T(8,128)(2,1)}, bf16[1,1024]{1,0:T(2,128)(2,1)}) custom-call(bf16[48,4096]{1,0:T(8,128)(2,1)S(1)} %copy-done, bf16[1,1024]{1,0:T(2,128)(2,1)S(1)} %copy-done.1), custom_call_target="tpu_custom_call" | custom-call | tf_op jit(solution)/shard_map/pallas_call | solution.py:375
Async XLA Ops:
  44.9 1.0 %copy-start = (bf16[48,4096]{1,0:T(8,128)(2,1)S(1)}, bf16[48,4096]{1,0:T(8,128)(2,1)}, u32[]{:S(2)}) copy-start(bf16[48,4096]{1,0:T(8,128)(2,1)} %get-tuple-element.4.layer_in) | copy-start | bytes 1179652
  45.9 0.7 %copy-start.1 = (bf16[1,1024]{1,0:T(2,128)(2,1)S(1)}, bf16[1,1024]{1,0:T(2,128)(2,1)}, u32[]{:S(2)}) copy-start(bf16[1,1024]{1,0:T(2,128)(2,1)} %get-tuple-element.5.dec_in) | copy-start | bytes 6148
